TPU v7x, 256 devices: a whole 4x4x8 slice. The times are simulated.
256 devices in a mesh: dp: 64 (over z, x, y_lo), mp: 4 (over y_hi, core).
Axes of the slice: x: 4, y: 4 (y_hi: 2, y_lo: 2; y = y_hi * 2 + y_lo), z: 8, core: 2. Of those that a mesh axis runs over, the one named last changes fastest.
Arguments:
- patches: bfloat16 [32768, 2048], P('dp'), may hold values from -16 to 16
- cotangent: bfloat16 [32768, 8192], P('dp', 'mp'), may hold values from -0.03125 to 0.03125
- weight: float32 [2048, 8192], P('dp', 'mp'), may hold values from -0.125 to 0.125
- accum: float32 [2048, 8192], P('dp', 'mp'), may hold values from 0.1 to 4
Outputs:
- new_weight: float32 [2048, 8192], P(('dp', 'mp'))
- new_accum: float32 [2048, 8192], P(('dp', 'mp'))
- weight_copy: bfloat16 [2048, 8192], P(None, 'mp')
All inputs are finite; a program needn't handle non-finite values.
Results may differ from a plain program's by a relative error of at most 0.001.
Values may be sent and summed in bfloat16 or wider, within the bound.
No kernel may reach another device: no remote copies, remote signals or barrier semaphores. Data moves between devices by JAX's collectives and lax.ppermute only.
A program may use at most 192 MiB of HBM per device.

v0:
```python
import jax
import jax.numpy as jnp
from jax import lax
from jax.sharding import Mesh
from jax.sharding import PartitionSpec as P

DP = ("dp_0", "dp_1", "dp_2")
DP_MP = ("dp_0", "dp_1", "dp_2", "mp")


learning_rate = 0.02


def sum_by_axis(running, axes):
    for axis in axes:
        running = lax.psum_scatter(running, axis, scatter_dimension=0, tiled=True)
    return running


def in_order(blocks, dim):
    blocks = jnp.moveaxis(blocks, 0, dim)
    shape = blocks.shape
    return blocks.reshape(*shape[:dim], shape[dim] * shape[dim + 1], *shape[dim + 2 :])


def gather_in_order(value, axes, turns):
    blocks = value
    for k in turns:
        blocks = lax.all_gather(blocks, axes[k])
    done = turns[::-1]
    back = [done.index(k) for k in range(len(axes))]
    blocks = blocks.transpose(*back, *range(len(axes), blocks.ndim))
    return blocks.reshape(-1, *value.shape)


def gathered_by_axis(value, axes, turns, dim):
    return in_order(gather_in_order(value, axes, turns), dim)


def adagrad(accum, weight, grad):
    summed = accum + grad * grad
    return (summed, weight - learning_rate * grad * lax.rsqrt(summed))


def shards(patches, cotangent, weight, accum):
    grad_block = sum_by_axis(
        jnp.einsum("tr,tf->rf", patches, cotangent, preferred_element_type=jnp.float32), DP
    )
    accum_block, weight_block = adagrad(accum, weight, grad_block)
    weight_copy = gathered_by_axis(weight_block.astype(jnp.bfloat16), DP, (2, 0, 1), 0)
    new_accum, new_weight = (
        lax.all_to_all(accum_block, "mp", split_axis=0, concat_axis=1, tiled=True),
        lax.all_to_all(weight_block, "mp", split_axis=0, concat_axis=1, tiled=True),
    )
    return (new_weight, new_accum, weight_copy)


def solution(mesh):
    finer = Mesh(mesh.devices.reshape(8, 4, 2, mesh.shape["mp"]), ("dp_0", "dp_1", "dp_2", "mp"))
    placed = (P(DP, None), P(DP, "mp"), P(DP, "mp"), P(DP, "mp"))
    return jax.shard_map(
        shards,
        mesh=finer,
        in_specs=placed,
        out_specs=(P(DP_MP, None), P(DP_MP, None), P(None, "mp")),
        check_vma=False,
    )
```

profile of v0, /device:TPU:1, one launch (start us, length us, event | category | flops | bytes accessed | tf_op | source)
XLA Modules:
  0.0 403.1 jit_solution(13332053273136321482)
XLA Ops:
  7.2 0.0 copy-start
  7.2 0.0 reduce-scatter.4.cloned.1.call-start
  7.2 1.5 copy-done
  8.8 9.7 %fusion.3 = f32[2048,2048]{1,0:T(8,128)} fusion(bf16[512,2048]{1,0:T(8,128)(2,1)S(1)} %copy-done, bf16[512,2048]{1,0:T(8,128)(2,1)} %param.5), kind=kOutput, calls=%fused_computation.5 | convolution fusion | flops 4294967296 | bytes 20971520 | tf_op jit(solution)/shard_map/tr,tf->rf/dot_general | solution.py:47
  18.5 0.0 reduce-scatter.4.cloned.1.call-update
  18.5 0.0 copy-start.1
  18.5 0.0 copy-start.2
  18.5 0.0 reduce-scatter.6.cloned.1.call-start
  18.6 177.4 %reduce-scatter.4.cloned.1.call-done = f32[256,2048]{1,0:T(8,128)} async-done(((f32[2048,2048]{1,0:T(8,128)}), f32[256,2048]{1,0:T(8,128)}) %reduce-scatter.4.cloned.1.call-update) | async-done | bytes 2097168 | tf_op jit(solution)/shard_map/reduce_scatter | solution.py:16
  195.9 0.0 reduce-scatter.6.cloned.1.call-update
  196.0 0.0 reduce-scatter.8.cloned.1.call-start
  196.0 33.4 %reduce-scatter.6.cloned.1.call-done = f32[64,2048]{1,0:T(8,128)} async-done(((f32[256,2048]{1,0:T(8,128)}), f32[64,2048]{1,0:T(8,128)}) %reduce-scatter.6.cloned.1.call-update) | async-done | bytes 524304 | tf_op jit(solution)/shard_map/reduce_scatter | solution.py:16
  229.4 0.0 reduce-scatter.8.cloned.1.call-update
  229.4 0.0 all-gather.6.cloned.1.call-start
  229.5 21.9 %reduce-scatter.8.cloned.1.call-done = f32[32,2048]{1,0:T(8,128)} async-done(((f32[64,2048]{1,0:T(8,128)}), f32[32,2048]{1,0:T(8,128)}) %reduce-scatter.8.cloned.1.call-update) | async-done | bytes 262160 | tf_op jit(solution)/shard_map/reduce_scatter | solution.py:16
  251.3 0.0 copy-done.1
  251.3 0.0 copy-done.2
  251.3 1.7 fusion.1
  253.0 5.0 %all-gather = bf16[64,2048]{1,0:T(8,128)(2,1)} all-gather(bf16[32,2048]{1,0:T(8,128)(2,1)S(1)} %get-tuple-element.3), channel_id=2, replica_groups=mesh['dp_0'=8,'dp_1'=4,'dp_2'=2,'mp'=4] {'dp_2'}, dimensions={0}, use_global_device_ids=true | all-gather | bytes 393216 | tf_op jit(solution)/shard_map/all_gather | solution.py:29
  258.0 0.0 all-gather.6.cloned.1.call-update
  258.1 0.0 all-gather.8.cloned.1.call-start
  258.1 38.8 %all-gather.6.cloned.1.call-done = bf16[16,32,2048]{2,1,0:T(8,128)(2,1)} async-done(((bf16[2,32,2048]{2,1,0:T(8,128)(2,1)}), bf16[16,32,2048]{2,1,0:T(8,128)(2,1)}) %all-gather.6.cloned.1.call-update) | async-done | bytes 2097168 | tf_op jit(solution)/shard_map/all_gather | solution.py:29
  296.9 0.0 all-gather.8.cloned.1.call-update
  296.9 15.4 %all_to_all.38 = f32[4,8,2048]{2,1,0:T(8,128)S(1)} all-to-all(f32[4,8,2048]{2,1,0:T(8,128)S(1)} %get-tuple-element.4), channel_id=1, replica_groups=mesh['dp_0'=8,'dp_1'=4,'dp_2'=2,'mp'=4] {'mp'}, dimensions={0} | all-to-all | bytes 524288 | tf_op jit(solution)/shard_map/all_to_all | solution.py:53
  312.3 4.4 %all-to-all-start.1 = ((f32[4,8,2048]{2,1,0:T(8,128)}), f32[4,8,2048]{2,1,0:T(8,128)S(1)}, u32[]{:S(2)}, u32[]{:S(2)}) async-start(f32[4,8,2048]{2,1,0:T(8,128)} %get-tuple-element.5), calls=%async_computation.4 | async-start | bytes 524288 | tf_op jit(solution)/shard_map/all_to_all | solution.py:52
  316.7 6.5 %all-to-all-done.1 = f32[4,8,2048]{2,1,0:T(8,128)S(1)} async-done(((f32[4,8,2048]{2,1,0:T(8,128)}), f32[4,8,2048]{2,1,0:T(8,128)S(1)}, u32[]{:S(2)}, u32[]{:S(2)}) %all-to-all-start.1) | async-done | bytes 262176 | tf_op jit(solution)/shard_map/all_to_all | solution.py:52
  323.3 63.4 %all-gather.8.cloned.1.call-done = bf16[32,2,32,2048]{3,2,1,0:T(8,128)(2,1)} async-done(((bf16[8,2,32,2048]{3,2,1,0:T(8,128)(2,1)}), bf16[32,2,32,2048]{3,2,1,0:T(8,128)(2,1)}) %all-gather.8.cloned.1.call-update) | async-done | bytes 8388624 | tf_op jit(solution)/shard_map/all_gather | solution.py:29
  386.7 8.4 %copy.8 = bf16[8,4,2,32,2048]{4,3,2,1,0:T(8,128)(2,1)} copy(bf16[8,4,2,32,2048]{4,3,2,0,1:T(8,128)(2,1)} %bitcast.18) | data formatting | bytes 16777216 | tf_op jit(solution)/shard_map/transpose | solution.py:32
  395.2 0.7 copy.11
  395.9 0.7 copy.12
Async XLA Ops:
  7.2 1.6 copy-start
  7.2 188.8 %reduce-scatter.4.cloned.1.call-start = ((), (), s32[]{:S(2)}) async-start(), calls=%async_computation.5 | async-start | bytes 18874368 | tf_op jit(solution)/shard_map/reduce_scatter | solution.py:16
  18.5 232.8 %copy-start.1 = (f32[32,2048]{1,0:T(8,128)S(1)}, f32[32,2048]{1,0:T(8,128)}, u32[]{:S(2)}) copy-start(f32[32,2048]{1,0:T(8,128)} %param.6) | copy-start | bytes 786436
  18.5 232.8 %copy-start.2 = (f32[32,2048]{1,0:T(8,128)S(1)}, f32[32,2048]{1,0:T(8,128)}, u32[]{:S(2)}) copy-start(f32[32,2048]{1,0:T(8,128)} %param.7) | copy-start | bytes 786436
  18.5 210.9 %reduce-scatter.6.cloned.1.call-start = ((), (), s32[]{:S(2)}) async-start(), calls=%async_computation.6 | async-start | bytes 2621440 | tf_op jit(solution)/shard_map/reduce_scatter | solution.py:16
  196.0 55.4 %reduce-scatter.8.cloned.1.call-start = ((), (), s32[]{:S(2)}) async-start(), calls=%async_computation.7 | async-start | bytes 786432 | tf_op jit(solution)/shard_map/reduce_scatter | solution.py:16
  229.4 67.5 %all-gather.6.cloned.1.call-start = ((), (), s32[]{:S(2)}) async-start(), calls=%async_computation.8 | async-start | bytes 2359296 | tf_op jit(solution)/shard_map/all_gather | solution.py:29
  258.1 128.7 %all-gather.8.cloned.1.call-start = ((), (), s32[]{:S(2)}) async-start(), calls=%async_computation.9 | async-start | bytes 10485760 | tf_op jit(solution)/shard_map/all_gather | solution.py:29
  312.3 11.0 %all-to-all-start.1 = ((f32[4,8,2048]{2,1,0:T(8,128)}), f32[4,8,2048]{2,1,0:T(8,128)S(1)}, u32[]{:S(2)}, u32[]{:S(2)}) async-start(f32[4,8,2048]{2,1,0:T(8,128)} %get-tuple-element.5), calls=%async_computation.4 | async-start | bytes 524288 | tf_op jit(solution)/shard_map/all_to_all | solution.py:52
Sparse Core Ops, SparseCore 0:
  18.6 177.2 reduce-scatter.3
  198.5 30.8 reduce-scatter.5
  231.9 19.3 reduce-scatter.7
  258.2 38.6 all-gather.5
  298.5 88.1 all-gather.7
where the time goes:
time: 403 us
  waiting for transfers between devices  341 us (85%)
  blocking collectives  20.4 us (5%)
  between operations  13.8 us (3%)
  local copies, waits for them, and re-layouts  11.4 us (3%)
  matrix products  9.71 us (2%)
  starting transfers between devices  4.63 us (1%)
    reduce_scatter x3, waiting for transfers between devices, sum_by_axis(): running = lax.psum_scatter(running, axis, scatter_dimension=0, tiled=True)  233 us
    all_gather x2, waiting for transfers between devices, gather_in_order(): blocks = lax.all_gather(blocks, axes[k])  102 us
    all_to_all x1, blocking collectives, shards(): lax.all_to_all(weight_block, 'mp', split_axis=0, concat_axis=1, tiled=True)  15.4 us
    dot_general x1, matrix products, shards(): jnp.einsum('tr,tf->rf', patches, cotangent, preferred_element_type=jnp.fl...  9.71 us
    transpose x1, local copies, waits for them, and re-layouts, gather_in_order(): blocks = blocks.transpose(*back, *range(len(axes), blocks.ndim))  8.44 us
  transfers between devices with their start and end apart: 6, of which 6 were waited for; matrix products, arithmetic and copies ran while one was open for 0% of the time, Pallas kernels for 0%

commit v1 on v0

v1 whole, which is shorter than its diff:
```python
import jax
import jax.numpy as jnp
from jax import lax
from jax.sharding import Mesh
from jax.sharding import PartitionSpec as P

DP = ("dp_0", "dp_1", "dp_2")
DP_MP = ("dp_0", "dp_1", "dp_2", "mp")


learning_rate = 0.02


def adagrad(accum, weight, grad):
    summed = accum + grad * grad
    return (summed, weight - learning_rate * grad * lax.rsqrt(summed))


def shards(patches, cotangent, weight, accum):
    partial = jnp.einsum("tr,tf->rf", patches, cotangent, preferred_element_type=jnp.float32)
    over_zx = lax.psum_scatter(partial, DP[:2], scatter_dimension=0, tiled=True)
    grad_block = lax.psum_scatter(over_zx, DP[2], scatter_dimension=0, tiled=True)
    accum_block, weight_block = adagrad(accum, weight, grad_block)
    pair = lax.all_gather(weight_block.astype(jnp.bfloat16), DP[2], axis=0, tiled=True)
    weight_copy = lax.all_gather(pair, DP[:2], axis=0, tiled=True)
    new_accum, new_weight = (
        lax.all_to_all(accum_block, "mp", split_axis=0, concat_axis=1, tiled=True),
        lax.all_to_all(weight_block, "mp", split_axis=0, concat_axis=1, tiled=True),
    )
    return (new_weight, new_accum, weight_copy)


def solution(mesh):
    finer = Mesh(mesh.devices.reshape(8, 4, 2, mesh.shape["mp"]), ("dp_0", "dp_1", "dp_2", "mp"))
    placed = (P(DP, None), P(DP, "mp"), P(DP, "mp"), P(DP, "mp"))
    return jax.shard_map(
        shards,
        mesh=finer,
        in_specs=placed,
        out_specs=(P(DP_MP, None), P(DP_MP, None), P(None, "mp")),
        check_vma=False,
    )
```

time: 403 us -> 413 us (1.025)
  waiting for transfers between devices: 341 us -> 355 us
    reduce_scatter x3 -> x2, waiting for transfers between devices: 233 us -> 272 us  [the longest x1 247 us: shards(): over_zx = lax.psum_scatter(partial, DP[:2], scatter_dimension=0, tiled=True)]
    all_gather x2 -> x1, waiting for transfers between devices: 102 us -> 76.4 us  [shards(): weight_copy = lax.all_gather(pair, DP[:2], axis=0, tiled=True)]
    transpose x1 -> x0, local copies, waits for them, and re-layouts: 8.44 us -> none  [gather_in_order(): blocks = blocks.transpose(*back, *range(len(axes), blocks.ndim))]
    unnamed x8 -> x9, local copies, waits for them, and re-layouts: 2.96 us -> 11.4 us
  transfers between devices with their start and end apart: 6 -> 4, of which waited for: 6 -> 4; matrix products, arithmetic and copies ran while one was open for 0% -> 0% of each run, Pallas kernels for 0% -> 0%
where the time goes in v1:
time: 413 us
  waiting for transfers between devices  355 us (86%)
  blocking collectives  16.9 us (4%)
  between operations  13.8 us (3%)
  local copies, waits for them, and re-layouts  11.4 us (3%)
  matrix products  9.71 us (2%)
  starting transfers between devices  4.54 us (1%)
    reduce_scatter x1, waiting for transfers between devices, shards(): over_zx = lax.psum_scatter(partial, DP[:2], scatter_dimension=0, tiled=True)  247 us
    all_gather x1, waiting for transfers between devices, shards(): weight_copy = lax.all_gather(pair, DP[:2], axis=0, tiled=True)  76.4 us
    reduce_scatter x1, waiting for transfers between devices, shards(): lax.psum_scatter(over_zx, DP[2], scatter_dimension=0, tiled=True)  24.8 us
    all_to_all x1, blocking collectives, shards(): lax.all_to_all(weight_block, 'mp', split_axis=0, concat_axis=1, tiled=True)  11.9 us
    unnamed x9, local copies, waits for them, and re-layouts  11.4 us
    dot_general x1, matrix products, shards(): jnp.einsum('tr,tf->rf', patches, cotangent, preferred_element_type=jnp.fl...  9.71 us
  transfers between devices with their start and end apart: 4, of which 4 were waited for; matrix products, arithmetic and copies ran while one was open for 0% of the time, Pallas kernels for 0%

profile of v1, /device:TPU:1, one launch (start us, length us, event | category | flops | bytes accessed | tf_op | source)
XLA Modules:
  0.0 412.8 jit_solution(9931146226808949405)
XLA Ops:
  7.2 0.0 copy-start
  7.2 0.0 reduce-scatter.3.cloned.1.call-start
  7.2 1.5 copy-done
  8.8 9.7 %fusion.3 = f32[2048,2048]{1,0:T(8,128)} fusion(bf16[512,2048]{1,0:T(8,128)(2,1)S(1)} %copy-done, bf16[512,2048]{1,0:T(8,128)(2,1)} %param.5), kind=kOutput, calls=%fused_computation.5 | convolution fusion | flops 4294967296 | bytes 20971520 | tf_op jit(solution)/shard_map/tr,tf->rf/dot_general | solution.py:20
  18.5 0.0 copy-start.1
  18.5 0.0 copy-start.2
  18.5 0.0 reduce-scatter.3.cloned.1.call-update
  18.5 0.0 reduce-scatter.5.cloned.1.call-start
  18.6 247.0 %reduce-scatter.3.cloned.1.call-done = f32[64,2048]{1,0:T(8,128)} async-done(((f32[2048,2048]{1,0:T(8,128)}), f32[64,2048]{1,0:T(8,128)}) %reduce-scatter.3.cloned.1.call-update) | async-done | bytes 524304 | tf_op jit(solution)/shard_map/reduce_scatter | solution.py:21
  265.6 0.0 reduce-scatter.5.cloned.1.call-update
  265.6 0.0 all-gather.2.cloned.1.call-start
  265.7 24.8 %reduce-scatter.5.cloned.1.call-done = f32[32,2048]{1,0:T(8,128)} async-done(((f32[64,2048]{1,0:T(8,128)}), f32[32,2048]{1,0:T(8,128)}) %reduce-scatter.5.cloned.1.call-update) | async-done | bytes 262160 | tf_op jit(solution)/shard_map/reduce_scatter | solution.py:22
  290.5 0.0 copy-done.1
  290.5 0.0 copy-done.2
  290.5 1.7 fusion.1
  292.2 5.0 %all_gather.6 = bf16[64,2048]{1,0:T(8,128)(2,1)} all-gather(bf16[32,2048]{1,0:T(8,128)(2,1)S(1)} %get-tuple-element.3), channel_id=1, replica_groups=mesh['dp_0'=8,'dp_1'=4,'dp_2'=2,'mp'=4] {'dp_2'}, dimensions={0}, use_global_device_ids=true | all-gather | bytes 393216 | tf_op jit(solution)/shard_map/all_gather | solution.py:24
  297.2 0.0 all-gather.2.cloned.1.call-update
  297.2 11.9 %all_to_all.38 = f32[4,8,2048]{2,1,0:T(8,128)S(1)} all-to-all(f32[4,8,2048]{2,1,0:T(8,128)S(1)} %get-tuple-element.4), channel_id=1, replica_groups=mesh['dp_0'=8,'dp_1'=4,'dp_2'=2,'mp'=4] {'mp'}, dimensions={0} | all-to-all | bytes 524288 | tf_op jit(solution)/shard_map/all_to_all | solution.py:28
  309.1 4.4 %all-to-all-start.1 = ((f32[4,8,2048]{2,1,0:T(8,128)}), f32[4,8,2048]{2,1,0:T(8,128)S(1)}, u32[]{:S(2)}, u32[]{:S(2)}) async-start(f32[4,8,2048]{2,1,0:T(8,128)} %get-tuple-element.5), calls=%async_computation.3 | async-start | bytes 524288 | tf_op jit(solution)/shard_map/all_to_all | solution.py:27
  313.5 6.5 %all-to-all-done.1 = f32[4,8,2048]{2,1,0:T(8,128)S(1)} async-done(((f32[4,8,2048]{2,1,0:T(8,128)}), f32[4,8,2048]{2,1,0:T(8,128)S(1)}, u32[]{:S(2)}, u32[]{:S(2)}) %all-to-all-start.1) | async-done | bytes 262176 | tf_op jit(solution)/shard_map/all_to_all | solution.py:27
  320.1 76.4 %all-gather.2.cloned.1.call-done = bf16[2048,2048]{1,0:T(8,128)(2,1)} async-done(((bf16[64,2048]{1,0:T(8,128)(2,1)}), bf16[2048,2048]{1,0:T(8,128)(2,1)}) %all-gather.2.cloned.1.call-update) | async-done | bytes 8388624 | tf_op jit(solution)/shard_map/all_gather | solution.py:25
  396.4 0.7 copy.10
  397.2 0.7 copy.11
  397.9 8.4 %copy.12 = bf16[2048,2048]{1,0:T(8,128)(2,1)} copy(bf16[2048,2048]{1,0:T(8,128)(2,1)} %all-gather.2.cloned.1.call-done) | data formatting | bytes 16777216
Async XLA Ops:
  7.2 1.6 copy-start
  7.2 258.4 %reduce-scatter.3.cloned.1.call-start = ((), (), s32[]{:S(2)}) async-start(), calls=%async_computation.4 | async-start | bytes 17301504 | tf_op jit(solution)/shard_map/reduce_scatter | solution.py:21
  18.5 272.0 %copy-start.1 = (f32[32,2048]{1,0:T(8,128)S(1)}, f32[32,2048]{1,0:T(8,128)}, u32[]{:S(2)}) copy-start(f32[32,2048]{1,0:T(8,128)} %param.6) | copy-start | bytes 786436
  18.5 272.0 %copy-start.2 = (f32[32,2048]{1,0:T(8,128)S(1)}, f32[32,2048]{1,0:T(8,128)}, u32[]{:S(2)}) copy-start(f32[32,2048]{1,0:T(8,128)} %param.7) | copy-start | bytes 786436
  18.5 272.0 %reduce-scatter.5.cloned.1.call-start = ((), (), s32[]{:S(2)}) async-start(), calls=%async_computation.5 | async-start | bytes 786432 | tf_op jit(solution)/shard_map/reduce_scatter | solution.py:22
  265.6 130.8 %all-gather.2.cloned.1.call-start = ((), (), s32[]{:S(2)}) async-start(), calls=%async_computation.6 | async-start | bytes 8650752 | tf_op jit(solution)/shard_map/all_gather | solution.py:25
  309.1 11.0 %all-to-all-start.1 = ((f32[4,8,2048]{2,1,0:T(8,128)}), f32[4,8,2048]{2,1,0:T(8,128)S(1)}, u32[]{:S(2)}, u32[]{:S(2)}) async-start(f32[4,8,2048]{2,1,0:T(8,128)} %get-tuple-element.5), calls=%async_computation.3 | async-start | bytes 524288 | tf_op jit(solution)/shard_map/all_to_all | solution.py:27
Sparse Core Ops, SparseCore 0:
  18.6 246.9 reduce-scatter.2
  268.1 22.3 reduce-scatter.4
  297.3 99.0 all-gather.1
